TPU v7x, 256 devices: a whole 4x4x8 slice. The times are simulated.
256 devices in a mesh: query: 8 (over y, z_hi), ctx: 32 (over x, z_lo, core).
Axes of the slice: x: 4, y: 4, z: 8 (z_hi: 2, z_lo: 4; z = z_hi * 4 + z_lo), core: 2. Of those that a mesh axis runs over, the one named last changes fastest.
Arguments:
- query_states: bfloat16 [256, 3072], P('query'), may hold values from -370 to 370
- key_states: bfloat16 [32768, 3072], P('ctx', 'query'), may hold values from -10.5 to 10.5
- value_states: bfloat16 [32768, 3072], P('ctx', 'query'), may hold values from -6 to 6
- level_ids: int32 [32768], P('ctx'), may hold values from 0 to 4, as said below
- level_bias: float32 [5, 24], replicated, may hold values from -1.5 to 1.5
- live_counts: int32 [32], P('ctx'), may hold values from 256 to 1024, as said below
- out_grad: bfloat16 [256, 3072], P('query'), may hold values from -6 to 6
Outputs:
- attn_out: bfloat16 [256, 3072], P(('query', 'ctx'))
- query_grad: bfloat16 [256, 3072], P(('query', 'ctx'))
- key_grad: bfloat16 [32768, 3072], P('ctx', 'query')
- value_grad: bfloat16 [32768, 3072], P('ctx', 'query')
Inputs may be any that keep to these rules, and one draw needn't show every extreme that they name: Owner c's slots c * 1024 to c * 1024 + live_counts[c] - 1 are live, its other slots are empty; at least one owner has all 1024 slots live. `level_ids`: constant over each aligned run of 16 slots.
All inputs are finite; a program needn't handle non-finite values.
Results may differ from a plain program's by a relative error of at most 0.012.
Values may be sent and summed in bfloat16 or wider, within the bound.
A program may use at most 64 MiB of HBM per device.

v0:
```python
import math
import jax
import jax.numpy as jnp
from jax import lax
from jax.sharding import PartitionSpec as P


def copy_for_each(x, axis):
    copies = jnp.broadcast_to(x, (lax.axis_size(axis), *x.shape))
    return lax.all_to_all(copies, axis, split_axis=0, concat_axis=0, tiled=True)


def over_copies(x, axis):
    return copy_for_each(x, axis).max(axis=0)


def split_up(x, dim, peers):
    dims = x.shape
    pieces = x.reshape(*dims[:dim], peers, dims[dim] // peers, *dims[dim + 1 :])
    return jnp.moveaxis(pieces, dim, 0)


def sum_at_owner(x, axis, dim):
    peers = lax.axis_size(axis)
    pieces = lax.all_to_all(split_up(x, dim, peers), axis, 0, 0, tiled=True)
    return jnp.sum(pieces, axis=0)


def gather_turned(arrays, axis, dims):
    turned = [jnp.moveaxis(a, dim, 0) for a, dim in zip(arrays, dims)]
    widths = [t[0].size for t in turned]
    both = jnp.concatenate([t.reshape(-1, w) for t, w in zip(turned, widths)], axis=1)
    out = lax.all_gather(both, axis, axis=0, tiled=True)
    pieces = jnp.split(out, [sum(widths[:k]) for k in range(1, len(widths))], axis=1)
    return tuple(
        (
            jnp.moveaxis(b.reshape(-1, *t.shape[1:]), 0, dim)
            for b, t, dim in zip(pieces, turned, dims)
        )
    )


def rescale(outputs, factor):
    row_count = outputs.shape[0]
    head_count = factor.shape[0]
    return (outputs.reshape(row_count, head_count, -1) * factor.T[:, :, None]).reshape(
        row_count, -1
    )


def local(query_states, key_states, value_states, level_ids, level_bias, live_counts, out_grad):
    query_ways = lax.axis_size("query")
    owner_ways = lax.axis_size("ctx")
    level_count, head_total = level_bias.shape
    moved_queries, moved_grads = (
        lax.all_to_all(query_states, "query", split_axis=1, concat_axis=0, tiled=True),
        lax.all_to_all(out_grad, "query", split_axis=1, concat_axis=0, tiled=True),
    )
    rows_total = moved_queries.shape[0]
    part_rows = rows_total // query_ways // owner_ways

    def regroup(array):
        return jnp.transpose(
            array.reshape(query_ways, owner_ways, part_rows, -1), (1, 0, 2, 3)
        ).reshape(rows_total, -1)

    queries_in = regroup(moved_queries)
    grads_in = regroup(moved_grads)
    key_full, value_full = (key_states, value_states)
    head_count = head_total // query_ways
    bias_table = lax.dynamic_slice_in_dim(
        level_bias, lax.axis_index("query") * head_count, head_count, 1
    )
    query_count, feature_count = queries_in.shape
    slot_count = key_full.shape[0]
    head_size = feature_count // head_count
    softmax_scale = 1.0 / math.sqrt(head_size)
    queries = queries_in.reshape(query_count, head_count, head_size)
    key_heads = key_full.reshape(slot_count, head_count, head_size)
    value_heads = value_full.reshape(slot_count, head_count, head_size)
    grad_heads = grads_in.reshape(query_count, head_count, head_size)
    live_slots = lax.broadcasted_iota(jnp.int32, (slot_count,), 0) < live_counts[0]
    level_onehot = (
        level_ids[:, None] == lax.broadcasted_iota(jnp.int32, (1, level_count), 1)
    ).astype(jnp.float32)
    level_term = jnp.dot(
        level_onehot,
        bias_table,
        precision=lax.Precision.HIGHEST,
        preferred_element_type=jnp.float32,
    )
    scores = (
        jnp.einsum("qhd,khd->hqk", queries, key_heads, preferred_element_type=jnp.float32)
        * softmax_scale
    )
    scores = jnp.where(live_slots[None, None, :], scores + level_term.T[:, None, :], -1e30)
    local_max = jnp.max(scores, axis=2)
    raw_weights = jnp.exp(scores - local_max[..., None])
    local_sum = jnp.sum(raw_weights, axis=2)
    partial_value = jnp.einsum(
        "hqk,khd->qhd",
        raw_weights.astype(jnp.bfloat16),
        value_heads,
        preferred_element_type=jnp.float32,
    ).reshape(query_count, feature_count)
    row_count = query_count // owner_ways
    row_start = lax.axis_index("ctx") * row_count
    row_peak = over_copies(local_max, "ctx")
    factor = jnp.exp(local_max - row_peak)
    out_rows, sum_rows = (
        sum_at_owner(rescale(partial_value, factor), "ctx", 0),
        sum_at_owner(local_sum * factor, "ctx", 1),
    )
    peak_rows = lax.dynamic_slice_in_dim(row_peak, row_start, row_count, 1)
    attention_rows = out_rows.reshape(row_count, head_count, head_size) / sum_rows.T[:, :, None]
    grad_rows = lax.dynamic_slice_in_dim(grad_heads, row_start, row_count, 0)
    delta_rows = jnp.sum(grad_rows * attention_rows, axis=2).T
    log_rows = peak_rows + jnp.log(sum_rows)
    log_total, deltas = gather_turned((log_rows, delta_rows), "ctx", (1, 1))
    attn_rows = attention_rows.reshape(row_count, feature_count).astype(jnp.bfloat16)
    probabilities = jnp.exp(scores - log_total[..., None])
    dprobs = jnp.einsum("qhd,khd->hqk", grad_heads, value_heads, preferred_element_type=jnp.float32)
    dscores = (probabilities * (dprobs - deltas[..., None])).astype(jnp.bfloat16)
    prob_rounded = probabilities.astype(jnp.bfloat16)
    query_part = softmax_scale * jnp.einsum(
        "hqk,khd->qhd", dscores, key_heads, preferred_element_type=jnp.float32
    ).reshape(query_count, feature_count)
    query_rows = sum_at_owner(query_part, "ctx", 0).astype(jnp.bfloat16)
    block_shape = (head_count, owner_ways, query_ways, part_rows, slot_count)
    row_shape = (owner_ways, query_ways, part_rows, head_count, head_size)
    key_blocks = softmax_scale * jnp.einsum(
        "hcbrk,cbrhd->bkhd",
        dscores.reshape(block_shape),
        queries.reshape(row_shape),
        preferred_element_type=jnp.float32,
    )
    value_blocks = jnp.einsum(
        "hcbrk,cbrhd->bkhd",
        prob_rounded.reshape(block_shape),
        grad_heads.reshape(row_shape),
        preferred_element_type=jnp.float32,
    )
    key_cols = jnp.sum(key_blocks.astype(jnp.bfloat16).astype(jnp.float32), axis=0).reshape(
        slot_count, feature_count
    )
    value_cols = jnp.sum(value_blocks.astype(jnp.bfloat16).astype(jnp.float32), axis=0).reshape(
        slot_count, feature_count
    )
    attn_final, query_final = (
        lax.all_to_all(attn_rows, "query", split_axis=0, concat_axis=1, tiled=True),
        lax.all_to_all(query_rows, "query", split_axis=0, concat_axis=1, tiled=True),
    )
    return (attn_final, query_final, key_cols.astype(jnp.bfloat16), value_cols.astype(jnp.bfloat16))


def solution(mesh):
    placed = (
        P("query", None),
        P("ctx", "query"),
        P("ctx", "query"),
        P("ctx"),
        P(),
        P("ctx"),
        P("query", None),
    )
    return jax.shard_map(
        local,
        mesh=mesh,
        in_specs=placed,
        out_specs=(
            P(("query", "ctx"), None),
            P(("query", "ctx"), None),
            P("ctx", "query"),
            P("ctx", "query"),
        ),
        check_vma=False,
    )
```

profile of v0, /device:TPU:1, one launch (start us, length us, event | category | flops | bytes accessed | tf_op | source)
XLA Modules:
  0.0 183.3 jit_solution(12638040741019976941)
XLA Ops:
  0.6 1.6 copy.228
  2.3 11.6 %all-to-all-start = ((bf16[32,8,384]{2,0,1:T(8,128)(2,1)}), bf16[32,8,384]{2,0,1:T(8,128)(2,1)S(1)}, u32[]{:S(2)}, u32[]{:S(2)}) async-start(bf16[32,8,384]{2,0,1:T(8,128)(2,1)} %bitcast.82), calls=%async_computation | async-start | bytes 393216 | tf_op jit(solution)/shard_map/all_to_all | solution.py:56
  13.9 2.3 %copy.174 = bf16[1024,384]{0,1:T(8,128)(2,1)} copy(bf16[1024,384]{1,0:T(8,128)(2,1)} %param.8) | data formatting | bytes 1572864 | tf_op args[1]
  18.1 5.7 %all-to-all-done = bf16[32,8,384]{2,0,1:T(8,128)(2,1)S(1)} async-done(((bf16[32,8,384]{2,0,1:T(8,128)(2,1)}), bf16[32,8,384]{2,0,1:T(8,128)(2,1)S(1)}, u32[]{:S(2)}, u32[]{:S(2)}) %all-to-all-start) | async-done | bytes 196640 | tf_op jit(solution)/shard_map/all_to_all | solution.py:56
  24.5 1.9 %fusion.29 = (f32[3,256]{1,0:T(4,128)S(1)}, f32[3,256,1024]{2,1,0:T(8,128)S(1)}) fusion(f32[3,1024]{1,0:T(4,128)S(1)} %fusion.17, bf16[1024,3,128]{0,2,1:T(8,128)(2,1)} %bitcast.91, bf16[256,3,128]{2,1,0:T(4,128)(2,1)S(1)} %reshape_reshape.9, pred[1024]{0:T(1024)(128)(4,1)S(1)} %iota_compare_fusion.2), kind=kOutput, calls=%fused_computation.47 | convolution fusion | flops 204471552 | bytes 4145152 | tf_op jit(solution)/shard_map/qhd,khd->hqk/dot_general | solution.py:93
  27.0 9.1 %all-to-all-start.1 = ((f32[32,3,256]{2,1,0:T(4,128)}), f32[32,3,256]{2,1,0:T(4,128)S(1)}, u32[]{:S(2)}, u32[]{:S(2)}) async-start(f32[32,3,256]{2,1,0:T(4,128)} %broadcast_in_dim.16), calls=%async_computation.1 | async-start | bytes 262144 | tf_op jit(solution)/shard_map/all_to_all | solution.py:10
  36.1 2.3 %copy.177 = bf16[1024,384]{0,1:T(8,128)(2,1)} copy(bf16[1024,384]{1,0:T(8,128)(2,1)} %param.9) | data formatting | bytes 1572864 | tf_op args[2]
  38.4 1.6 copy.227
  40.0 4.8 %all-to-all-done.1 = f32[32,3,256]{2,1,0:T(4,128)S(1)} async-done(((f32[32,3,256]{2,1,0:T(4,128)}), f32[32,3,256]{2,1,0:T(4,128)S(1)}, u32[]{:S(2)}, u32[]{:S(2)}) %all-to-all-start.1) | async-done | bytes 98336 | tf_op jit(solution)/shard_map/all_to_all | solution.py:10
  44.8 3.4 %all-to-all-start.5 = ((bf16[32,8,384]{2,0,1:T(8,128)(2,1)}), bf16[32,8,384]{2,0,1:T(8,128)(2,1)S(1)}, u32[]{:S(2)}, u32[]{:S(2)}) async-start(bf16[32,8,384]{2,0,1:T(8,128)(2,1)} %bitcast.81), calls=%async_computation.5 | async-start | bytes 393216 | tf_op jit(solution)/shard_map/all_to_all | solution.py:57
  49.9 8.3 %all-to-all-done.5 = bf16[32,8,384]{2,0,1:T(8,128)(2,1)S(1)} async-done(((bf16[32,8,384]{2,0,1:T(8,128)(2,1)}), bf16[32,8,384]{2,0,1:T(8,128)(2,1)S(1)}, u32[]{:S(2)}, u32[]{:S(2)}) %all-to-all-start.5) | async-done | bytes 196640 | tf_op jit(solution)/shard_map/all_to_all | solution.py:57
  58.2 6.1 %all-to-all-start.3 = ((f32[32,3,8]{2,1,0:T(4,128)}), f32[32,3,8]{2,1,0:T(4,128)S(1)}, u32[]{:S(2)}, u32[]{:S(2)}) async-start(f32[32,3,8]{2,1,0:T(4,128)} %copy.181), calls=%async_computation.3 | async-start | bytes 131072 | tf_op jit(solution)/shard_map/all_to_all | solution.py:25
  64.4 1.8 fusion.13
  67.3 2.0 %reshape_reshape.10 = f32[32,8,384]{2,1,0:T(8,128)} reshape(f32[256,3,128]{2,1,0:T(4,128)} %copy.180) | data formatting | bytes 786432 | tf_op jit(solution)/shard_map/reshape;reshape | solution.py:19
  69.3 2.9 %all-to-all-done.3 = f32[32,3,8]{2,1,0:T(4,128)S(1)} async-done(((f32[32,3,8]{2,1,0:T(4,128)}), f32[32,3,8]{2,1,0:T(4,128)S(1)}, u32[]{:S(2)}, u32[]{:S(2)}) %all-to-all-start.3) | async-done | bytes 3104 | tf_op jit(solution)/shard_map/all_to_all | solution.py:25
  72.8 4.8 %all-to-all-start.2 = ((f32[32,8,384]{2,1,0:T(8,128)}), f32[32,8,384]{2,1,0:T(8,128)S(1)}, u32[]{:S(2)}, u32[]{:S(2)}) async-start(f32[32,8,384]{2,1,0:T(8,128)} %reshape_reshape.10), calls=%async_computation.2 | async-start | bytes 786432 | tf_op jit(solution)/shard_map/all_to_all | solution.py:25
  77.6 1.7 copy.229
  79.3 1.7 reshape_reshape.11
  80.9 1.7 copy.185
  84.1 7.5 %all-to-all-done.2 = f32[32,8,384]{2,1,0:T(8,128)S(1)} async-done(((f32[32,8,384]{2,1,0:T(8,128)}), f32[32,8,384]{2,1,0:T(8,128)S(1)}, u32[]{:S(2)}, u32[]{:S(2)}) %all-to-all-start.2) | async-done | bytes 393248 | tf_op jit(solution)/shard_map/all_to_all | solution.py:25
  93.3 39.9 %all_gather.3 = f32[256,6]{1,0:T(8,128)S(1)} all-gather(f32[8,6]{1,0:T(8,128)S(1)} %copy.186), channel_id=1, replica_groups=mesh['query'=8,'ctx'=32] {'ctx'}, dimensions={0}, use_global_device_ids=true | all-gather | bytes 6336 | tf_op jit(solution)/shard_map/all_gather | solution.py:33
  133.4 2.1 %multiply_convert_fusion.1 = bf16[3,256,1024]{2,1,0:T(8,128)(2,1)S(1)} fusion(f32[3,256,1024]{2,1,0:T(8,128)S(1)} %get-tuple-element.41, bf16[256,3,128]{2,0,1:T(8,128)(2,1)} %copy.185, bf16[1024,3,128]{0,2,1:T(8,128)(2,1)} %bitcast.87, f32[3,256]{1,0:T(4,128)S(1)} %copy.190, f32[3,256]{1,0:T(4,128)S(1)} %copy.187), kind=kOutput, calls=%fused_computation.3 | convolution fusion | flops 204472320 | bytes 5707776 | tf_op jit(solution)/shard_map/qhd,khd->hqk/dot_general | solution.py:122
  138.4 2.0 %mul.66 = f32[32,8,384]{2,1,0:T(8,128)} reshape(f32[256,3,128]{2,1,0:T(4,128)} %copy.192) | data formatting | bytes 786432 | tf_op jit(solution)/shard_map/mul | solution.py:125
  140.4 3.8 %all-to-all-start.6 = ((f32[32,8,384]{2,1,0:T(8,128)}), f32[32,8,384]{2,1,0:T(8,128)S(1)}, u32[]{:S(2)}, u32[]{:S(2)}) async-start(f32[32,8,384]{2,1,0:T(8,128)} %mul.66), calls=%async_computation.6 | async-start | bytes 786432 | tf_op jit(solution)/shard_map/all_to_all | solution.py:25
  144.3 1.3 fusion.23
  148.2 6.0 %fusion = bf16[3,1024,128]{2,1,0:T(8,128)(2,1)} fusion(bf16[3,32,8,1024]{3,2,1,0:T(8,128)(2,1)} %bitcast.88, bf16[32,8,3,128]{3,1,2,0:T(8,128)(2,1)} %bitcast.94), kind=kOutput, calls=%fused_computation.1 | convolution fusion | flops 210370560 | bytes 2555904 | tf_op jit(solution)/shard_map/hcbrk,cbrhd->bkhd/dot_general | solution.py:131
  154.2 4.0 %all-to-all-done.6 = f32[32,8,384]{2,1,0:T(8,128)S(1)} async-done(((f32[32,8,384]{2,1,0:T(8,128)}), f32[32,8,384]{2,1,0:T(8,128)S(1)}, u32[]{:S(2)}, u32[]{:S(2)}) %all-to-all-start.6) | async-done | bytes 393248 | tf_op jit(solution)/shard_map/all_to_all | solution.py:25
  158.2 3.3 %all-to-all-start.4 = ((bf16[8,2,192]{2,1,0:T(2,128)(2,1)}), bf16[8,2,192]{2,1,0:T(2,128)(2,1)S(1)}, u32[]{:S(2)}, u32[]{:S(2)}) async-start(bf16[8,2,192]{2,1,0:T(2,128)(2,1)} %reshape.124), calls=%async_computation.4 | async-start | bytes 16384 | tf_op jit(solution)/shard_map/all_to_all | solution.py:150
  161.6 1.6 fusion.4
  164.7 5.8 %all-to-all-done.4 = bf16[8,2,192]{2,1,0:T(2,128)(2,1)S(1)} async-done(((bf16[8,2,192]{2,1,0:T(2,128)(2,1)}), bf16[8,2,192]{2,1,0:T(2,128)(2,1)S(1)}, u32[]{:S(2)}, u32[]{:S(2)}) %all-to-all-start.4) | async-done | bytes 6176 | tf_op jit(solution)/shard_map/all_to_all | solution.py:150
  170.5 3.3 %all-to-all-start.7 = ((bf16[8,2,192]{2,1,0:T(2,128)(2,1)}), bf16[8,2,192]{2,1,0:T(2,128)(2,1)S(1)}, u32[]{:S(2)}, u32[]{:S(2)}) async-start(bf16[8,2,192]{2,1,0:T(2,128)(2,1)} %reshape.126), calls=%async_computation.7 | async-start | bytes 16384 | tf_op jit(solution)/shard_map/all_to_all | solution.py:151
  173.8 4.2 %convert_reduce_fusion = bf16[3,1024,128]{2,1,0:T(8,128)(2,1)S(1)} fusion(bf16[3,32,8,1024]{3,2,1,0:T(8,128)(2,1)} %fusion.4, bf16[32,8,3,128]{3,1,2,0:T(8,128)(2,1)} %bitcast.96), kind=kOutput, calls=%fused_computation.2 | convolution fusion | flops 207224832 | bytes 2555904 | tf_op jit(solution)/shard_map/hcbrk,cbrhd->bkhd/dot_general | solution.py:137
  (55 shorter events, 21.6 us)
Async XLA Ops:
  0.6 16.2 %copy-start = (f32[5,24]{1,0:T(8,128)S(1)}, f32[5,24]{1,0:T(8,128)}, u32[]{:S(2)}) copy-start(f32[5,24]{1,0:T(8,128)} %param.11) | copy-start | bytes 1444
  2.3 21.5 %all-to-all-start = ((bf16[32,8,384]{2,0,1:T(8,128)(2,1)}), bf16[32,8,384]{2,0,1:T(8,128)(2,1)S(1)}, u32[]{:S(2)}, u32[]{:S(2)}) async-start(bf16[32,8,384]{2,0,1:T(8,128)(2,1)} %bitcast.82), calls=%async_computation | async-start | bytes 393216 | tf_op jit(solution)/shard_map/all_to_all | solution.py:56
  23.8 0.7 copy-start.3
  27.0 17.8 %all-to-all-start.1 = ((f32[32,3,256]{2,1,0:T(4,128)}), f32[32,3,256]{2,1,0:T(4,128)S(1)}, u32[]{:S(2)}, u32[]{:S(2)}) async-start(f32[32,3,256]{2,1,0:T(4,128)} %broadcast_in_dim.16), calls=%async_computation.1 | async-start | bytes 262144 | tf_op jit(solution)/shard_map/all_to_all | solution.py:10
  44.8 13.4 %all-to-all-start.5 = ((bf16[32,8,384]{2,0,1:T(8,128)(2,1)}), bf16[32,8,384]{2,0,1:T(8,128)(2,1)S(1)}, u32[]{:S(2)}, u32[]{:S(2)}) async-start(bf16[32,8,384]{2,0,1:T(8,128)(2,1)} %bitcast.81), calls=%async_computation.5 | async-start | bytes 393216 | tf_op jit(solution)/shard_map/all_to_all | solution.py:57
  58.2 11.0 %copy-start.5 = (bf16[32,8,384]{2,0,1:T(8,128)(2,1)}, bf16[32,8,384]{2,0,1:T(8,128)(2,1)S(1)}, u32[]{:S(2)}) copy-start(bf16[32,8,384]{2,0,1:T(8,128)(2,1)S(1)} %all-to-all-done.5) | copy-start | bytes 589828
  58.2 13.9 %all-to-all-start.3 = ((f32[32,3,8]{2,1,0:T(4,128)}), f32[32,3,8]{2,1,0:T(4,128)S(1)}, u32[]{:S(2)}, u32[]{:S(2)}) async-start(f32[32,3,8]{2,1,0:T(4,128)} %copy.181), calls=%async_computation.3 | async-start | bytes 131072 | tf_op jit(solution)/shard_map/all_to_all | solution.py:25
  72.2 0.6 copy-start.6
  72.8 18.8 %all-to-all-start.2 = ((f32[32,8,384]{2,1,0:T(8,128)}), f32[32,8,384]{2,1,0:T(8,128)S(1)}, u32[]{:S(2)}, u32[]{:S(2)}) async-start(f32[32,8,384]{2,1,0:T(8,128)} %reshape_reshape.10), calls=%async_computation.2 | async-start | bytes 786432 | tf_op jit(solution)/shard_map/all_to_all | solution.py:25
  83.5 0.7 copy-start.9
  133.4 3.9 %copy-start.7 = (f32[3,256]{1,0:T(4,128)}, f32[3,256]{1,0:T(4,128)S(1)}, u32[]{:S(2)}) copy-start(f32[3,256]{1,0:T(4,128)S(1)} %copy.187) | copy-start | bytes 9220
  133.4 3.3 %copy-start.2 = (bf16[1024,384]{0,1:T(8,128)(2,1)S(1)}, bf16[1024,384]{0,1:T(8,128)(2,1)}, u32[]{:S(2)}) copy-start(bf16[1024,384]{0,1:T(8,128)(2,1)} %copy.174) | copy-start | bytes 2359300
  135.6 1.2 copy-start.1
  140.4 17.8 %all-to-all-start.6 = ((f32[32,8,384]{2,1,0:T(8,128)}), f32[32,8,384]{2,1,0:T(8,128)S(1)}, u32[]{:S(2)}, u32[]{:S(2)}) async-start(f32[32,8,384]{2,1,0:T(8,128)} %mul.66), calls=%async_computation.6 | async-start | bytes 786432 | tf_op jit(solution)/shard_map/all_to_all | solution.py:25
  148.2 13.4 %copy-start.8 = (f32[3,256]{1,0:T(4,128)S(1)}, f32[3,256]{1,0:T(4,128)}, u32[]{:S(2)}) copy-start(f32[3,256]{1,0:T(4,128)} %copy-done.7) | copy-start | bytes 9220
  158.2 12.2 %all-to-all-start.4 = ((bf16[8,2,192]{2,1,0:T(2,128)(2,1)}), bf16[8,2,192]{2,1,0:T(2,128)(2,1)S(1)}, u32[]{:S(2)}, u32[]{:S(2)}) async-start(bf16[8,2,192]{2,1,0:T(2,128)(2,1)} %reshape.124), calls=%async_computation.4 | async-start | bytes 16384 | tf_op jit(solution)/shard_map/all_to_all | solution.py:150
  163.2 14.7 %copy-start.4 = (bf16[3,1024,128]{2,1,0:T(8,128)(2,1)S(1)}, bf16[3,1024,128]{2,1,0:T(8,128)(2,1)}, u32[]{:S(2)}) copy-start(bf16[3,1024,128]{2,1,0:T(8,128)(2,1)} %fusion) | copy-start | bytes 2359300
  170.5 12.2 %all-to-all-start.7 = ((bf16[8,2,192]{2,1,0:T(2,128)(2,1)}), bf16[8,2,192]{2,1,0:T(2,128)(2,1)S(1)}, u32[]{:S(2)}, u32[]{:S(2)}) async-start(bf16[8,2,192]{2,1,0:T(2,128)(2,1)} %reshape.126), calls=%async_computation.7 | async-start | bytes 16384 | tf_op jit(solution)/shard_map/all_to_all | solution.py:151
where the time goes:
time: 185 us; the launch traced here: 183 us
  starting transfers between devices  45.6 us (25%)
  waiting for transfers between devices  40 us (22%)
  blocking collectives  39.9 us (22%)
  local copies, waits for them, and re-layouts  29.4 us (16%)
  matrix products  17.8 us (10%)
  other arithmetic  9.17 us (5%)
    all_gather x1, blocking collectives, gather_turned(): out = lax.all_gather(both, axis, axis=0, tiled=True)  39.9 us
    all_to_all x3, starting transfers between devices, sum_at_owner(): pieces = lax.all_to_all(split_up(x, dim, peers), axis, 0, 0, tiled=True)  14.8 us
    all_to_all x3, waiting for transfers between devices, sum_at_owner(): pieces = lax.all_to_all(split_up(x, dim, peers), axis, 0, 0, tiled=True)  14.4 us
    unnamed x28, local copies, waits for them, and re-layouts  12 us
    all_to_all x1, starting transfers between devices, local(): lax.all_to_all(query_states, 'query', split_axis=1, concat_axis=0, tiled=...  11.6 us
    all_to_all x1, starting transfers between devices, copy_for_each(): return lax.all_to_all(copies, axis, split_axis=0, concat_axis=0, tiled=True)  9.11 us
    all_to_all x1, waiting for transfers between devices, local(): lax.all_to_all(out_grad, 'query', split_axis=1, concat_axis=0, tiled=True)  8.29 us
    dot_general x1, matrix products, local(): jnp.einsum('hcbrk,cbrhd->bkhd', dscores.reshape(block_shape), queries.res...  6.05 us
  transfers between devices with their start and end apart: 8, of which 8 were waited for; matrix products, arithmetic and copies ran while one was open for 23% of the time, Pallas kernels for 0%

commit v1 on v0

--- a/solution.py
+++ b/solution.py
@@ -30,7 +30,9 @@
     turned = [jnp.moveaxis(a, dim, 0) for a, dim in zip(arrays, dims)]
     widths = [t[0].size for t in turned]
     both = jnp.concatenate([t.reshape(-1, w) for t, w in zip(turned, widths)], axis=1)
-    out = lax.all_gather(both, axis, axis=0, tiled=True)
+    out = jnp.concatenate(
+        lax.all_to_all(jnp.stack([both] * lax.axis_size(axis)), axis, 0, 0), axis=0
+    )
     pieces = jnp.split(out, [sum(widths[:k]) for k in range(1, len(widths))], axis=1)
     return tuple(
         (

time: 185 us -> 156 us (0.84)
  blocking collectives: 39.9 us -> 0 us
  starting transfers between devices: 45.6 us -> 53.5 us
  waiting for transfers between devices: 40 us -> 46.7 us
  matrix products: 17.8 us -> 15.7 us
    all_gather x1 -> x0, blocking collectives: 39.9 us -> none  [gather_turned(): out = lax.all_gather(both, axis, axis=0, tiled=True)]
    all_to_all x0 -> x1, waiting for transfers between devices: none -> 6.17 us  [gather_turned(): lax.all_to_all(jnp.stack([both] * lax.axis_size(axis)), axis, 0, 0)]
    all_to_all x1, waiting for transfers between devices: 5.79 us -> 1.77 us  [local(): lax.all_to_all(attn_rows, 'query', split_axis=0, concat_axis=1, tiled=True)]
    all_to_all x3, waiting for transfers between devices: 14.4 us -> 18 us  [sum_at_owner(): pieces = lax.all_to_all(split_up(x, dim, peers), axis, 0, 0, tiled=True)]
    all_to_all x0 -> x1, starting transfers between devices: none -> 3.64 us  [gather_turned(): lax.all_to_all(jnp.stack([both] * lax.axis_size(axis)), axis, 0, 0)]
    all_to_all x1, starting transfers between devices: 3.32 us -> 6.33 us  [local(): lax.all_to_all(query_rows, 'query', split_axis=0, concat_axis=1, tiled=True)]
    dot_general x1, matrix products: 6.05 us -> 4.07 us  [local(): jnp.einsum('hcbrk,cbrhd->bkhd', dscores.reshape(block_shape), queries.res...]
    unnamed x28 -> x32, local copies, waits for them, and re-layouts: 12 us -> 12.1 us
  transfers between devices with their start and end apart: 8 -> 9, of which waited for: 8 -> 9; matrix products, arithmetic and copies ran while one was open for 23% -> 27% of each run, Pallas kernels for 0% -> 0%
where the time goes in v1:
time: 156 us; the launch traced here: 155 us
  starting transfers between devices  53.5 us (34%)
  waiting for transfers between devices  46.7 us (30%)
  local copies, waits for them, and re-layouts  29.9 us (19%)
  matrix products  15.7 us (10%)
  other arithmetic  7.69 us (5%)
    all_to_all x3, waiting for transfers between devices, sum_at_owner(): pieces = lax.all_to_all(split_up(x, dim, peers), axis, 0, 0, tiled=True)  18 us
    all_to_all x3, starting transfers between devices, sum_at_owner(): pieces = lax.all_to_all(split_up(x, dim, peers), axis, 0, 0, tiled=True)  16 us
    unnamed x32, local copies, waits for them, and re-layouts  12.1 us
    all_to_all x1, starting transfers between devices, local(): lax.all_to_all(query_states, 'query', split_axis=1, concat_axis=0, tiled=...  11.6 us
    all_to_all x1, starting transfers between devices, copy_for_each(): return lax.all_to_all(copies, axis, split_axis=0, concat_axis=0, tiled=True)  9.11 us
    all_to_all x1, waiting for transfers between devices, local(): lax.all_to_all(out_grad, 'query', split_axis=1, concat_axis=0, tiled=True)  8.29 us
    all_to_all x1, starting transfers between devices, local(): lax.all_to_all(query_rows, 'query', split_axis=0, concat_axis=1, tiled=True)  6.33 us
    all_to_all x1, waiting for transfers between devices, gather_turned(): lax.all_to_all(jnp.stack([both] * lax.axis_size(axis)), axis, 0, 0)  6.17 us
  transfers between devices with their start and end apart: 9, of which 9 were waited for; matrix products, arithmetic and copies ran while one was open for 27% of the time, Pallas kernels for 0%

profile of v1, /device:TPU:1, one launch (start us, length us, event | category | flops | bytes accessed | tf_op | source)
XLA Modules:
  0.0 155.0 jit_solution(530626293258355828)
XLA Ops:
  0.6 1.6 %copy.183 = bf16[4,8,8,384]{3,2,0,1:T(8,128)(2,1)} copy(bf16[4,8,8,384]{3,2,1,0:T(8,128)(2,1)} %bitcast.101) | data formatting | bytes 393216 | tf_op jit(solution)/shard_map/all_to_all | solution.py:58
  2.3 11.6 %all-to-all-start = ((bf16[32,8,384]{2,0,1:T(8,128)(2,1)}), bf16[32,8,384]{2,0,1:T(8,128)(2,1)S(1)}, u32[]{:S(2)}, u32[]{:S(2)}) async-start(bf16[32,8,384]{2,0,1:T(8,128)(2,1)} %bitcast.84), calls=%async_computation | async-start | bytes 393216 | tf_op jit(solution)/shard_map/all_to_all | solution.py:58
  13.9 2.3 %copy.131 = bf16[1024,384]{0,1:T(8,128)(2,1)} copy(bf16[1024,384]{1,0:T(8,128)(2,1)} %param.8) | data formatting | bytes 1572864 | tf_op args[1]
  18.1 5.7 %all-to-all-done = bf16[32,8,384]{2,0,1:T(8,128)(2,1)S(1)} async-done(((bf16[32,8,384]{2,0,1:T(8,128)(2,1)}), bf16[32,8,384]{2,0,1:T(8,128)(2,1)S(1)}, u32[]{:S(2)}, u32[]{:S(2)}) %all-to-all-start) | async-done | bytes 196640 | tf_op jit(solution)/shard_map/all_to_all | solution.py:58
  24.5 1.9 %fusion.29 = (f32[3,256]{1,0:T(4,128)S(1)}, f32[3,256,1024]{2,1,0:T(8,128)S(1)}) fusion(f32[3,1024]{1,0:T(4,128)S(1)} %fusion.17, bf16[1024,3,128]{0,2,1:T(8,128)(2,1)} %bitcast.93, bf16[256,3,128]{2,1,0:T(4,128)(2,1)S(1)} %reshape_reshape.9, pred[1024]{0:T(1024)(128)(4,1)S(1)} %iota_compare_fusion.2), kind=kOutput, calls=%fused_computation.47 | convolution fusion | flops 204471552 | bytes 4145152 | tf_op jit(solution)/shard_map/qhd,khd->hqk/dot_general | solution.py:95
  27.1 9.1 %all-to-all-start.1 = ((f32[32,3,256]{2,1,0:T(4,128)}), f32[32,3,256]{2,1,0:T(4,128)S(1)}, u32[]{:S(2)}, u32[]{:S(2)}) async-start(f32[32,3,256]{2,1,0:T(4,128)} %broadcast_in_dim.16), calls=%async_computation.1 | async-start | bytes 262144 | tf_op jit(solution)/shard_map/all_to_all | solution.py:10
  36.2 2.3 %copy.134 = bf16[1024,384]{0,1:T(8,128)(2,1)} copy(bf16[1024,384]{1,0:T(8,128)(2,1)} %param.9) | data formatting | bytes 1572864 | tf_op args[2]
  40.1 4.8 %all-to-all-done.1 = f32[32,3,256]{2,1,0:T(4,128)S(1)} async-done(((f32[32,3,256]{2,1,0:T(4,128)}), f32[32,3,256]{2,1,0:T(4,128)S(1)}, u32[]{:S(2)}, u32[]{:S(2)}) %all-to-all-start.1) | async-done | bytes 98336 | tf_op jit(solution)/shard_map/all_to_all | solution.py:10
  44.9 3.4 %all-to-all-start.5 = ((bf16[32,8,384]{2,0,1:T(8,128)(2,1)}), bf16[32,8,384]{2,0,1:T(8,128)(2,1)S(1)}, u32[]{:S(2)}, u32[]{:S(2)}) async-start(bf16[32,8,384]{2,0,1:T(8,128)(2,1)} %bitcast.83), calls=%async_computation.5 | async-start | bytes 393216 | tf_op jit(solution)/shard_map/all_to_all | solution.py:59
  50.0 8.3 %all-to-all-done.5 = bf16[32,8,384]{2,0,1:T(8,128)(2,1)S(1)} async-done(((bf16[32,8,384]{2,0,1:T(8,128)(2,1)}), bf16[32,8,384]{2,0,1:T(8,128)(2,1)S(1)}, u32[]{:S(2)}, u32[]{:S(2)}) %all-to-all-start.5) | async-done | bytes 196640 | tf_op jit(solution)/shard_map/all_to_all | solution.py:59
  58.3 6.1 %all-to-all-start.3 = ((f32[32,3,8]{2,1,0:T(4,128)}), f32[32,3,8]{2,1,0:T(4,128)S(1)}, u32[]{:S(2)}, u32[]{:S(2)}) async-start(f32[32,3,8]{2,1,0:T(4,128)} %copy.138), calls=%async_computation.3 | async-start | bytes 131072 | tf_op jit(solution)/shard_map/all_to_all | solution.py:25
  64.4 1.8 %fusion.13 = f32[256,3,128]{2,0,1:T(8,128)S(1)} fusion(bf16[1024,3,128]{0,2,1:T(8,128)(2,1)} %bitcast.88, f32[3,256,1024]{2,1,0:T(8,128)S(1)} %get-tuple-element.37, f32[3,256]{1,0:T(4,128)S(1)} %get-tuple-element.36, f32[256,3]{0,1:T(4,128)S(1)} %get-tuple-element.35), kind=kOutput, calls=%fused_computation.16 | convolution fusion | flops 202997760 | bytes 4331520 | tf_op jit(solution)/shard_map/hqk,khd->qhd/dot_general | solution.py:102
  67.3 2.0 %reshape_reshape.10 = f32[32,8,384]{2,1,0:T(8,128)} reshape(f32[256,3,128]{2,1,0:T(4,128)} %copy.137) | data formatting | bytes 786432 | tf_op jit(solution)/shard_map/reshape;reshape | solution.py:19
  69.3 2.9 %all-to-all-done.3 = f32[32,3,8]{2,1,0:T(4,128)S(1)} async-done(((f32[32,3,8]{2,1,0:T(4,128)}), f32[32,3,8]{2,1,0:T(4,128)S(1)}, u32[]{:S(2)}, u32[]{:S(2)}) %all-to-all-start.3) | async-done | bytes 3104 | tf_op jit(solution)/shard_map/all_to_all | solution.py:25
  72.8 4.8 %all-to-all-start.2 = ((f32[32,8,384]{2,1,0:T(8,128)}), f32[32,8,384]{2,1,0:T(8,128)S(1)}, u32[]{:S(2)}, u32[]{:S(2)}) async-start(f32[32,8,384]{2,1,0:T(8,128)} %reshape_reshape.10), calls=%async_computation.2 | async-start | bytes 786432 | tf_op jit(solution)/shard_map/all_to_all | solution.py:25
  77.7 1.7 %copy.184 = bf16[32,8,384]{2,1,0:T(8,128)(2,1)} copy(bf16[32,8,384]{2,0,1:T(8,128)(2,1)} %copy-done.9) | data formatting | bytes 393216 | tf_op jit(solution)/shard_map/all_to_all | solution.py:59
  79.3 1.7 %reshape_reshape.11 = bf16[256,3,128]{2,1,0:T(4,128)(2,1)} reshape(bf16[32,8,1,384]{3,1,0,2:T(8,128)(2,1)} %bitcast.97) | data formatting | bytes 393216 | tf_op jit(solution)/shard_map/reshape;reshape | solution.py:83
  81.0 1.7 %copy.142 = bf16[256,3,128]{2,0,1:T(8,128)(2,1)} copy(bf16[256,3,128]{2,1,0:T(4,128)(2,1)} %reshape_reshape.11) | data formatting | bytes 393216 | tf_op jit(solution)/shard_map/reshape;reshape | solution.py:83
  84.2 7.5 %all-to-all-done.2 = f32[32,8,384]{2,1,0:T(8,128)S(1)} async-done(((f32[32,8,384]{2,1,0:T(8,128)}), f32[32,8,384]{2,1,0:T(8,128)S(1)}, u32[]{:S(2)}, u32[]{:S(2)}) %all-to-all-start.2) | async-done | bytes 393248 | tf_op jit(solution)/shard_map/all_to_all | solution.py:25
  93.9 3.6 %all-to-all-start.6 = ((f32[32,8,6]{1,2,0:T(8,128)}), f32[32,8,6]{1,2,0:T(8,128)S(1)}, u32[]{:S(2)}, u32[]{:S(2)}) async-start(f32[32,8,6]{1,2,0:T(8,128)} %stack.2), calls=%async_computation.6 | async-start | bytes 262144 | tf_op jit(solution)/shard_map/all_to_all | solution.py:34
  100.1 6.2 %all-to-all-done.6 = f32[32,8,6]{1,2,0:T(8,128)S(1)} async-done(((f32[32,8,6]{1,2,0:T(8,128)}), f32[32,8,6]{1,2,0:T(8,128)S(1)}, u32[]{:S(2)}, u32[]{:S(2)}) %all-to-all-start.6) | async-done | bytes 6176 | tf_op jit(solution)/shard_map/all_to_all | solution.py:34
  106.3 3.3 %all-to-all-start.4 = ((bf16[8,2,192]{2,1,0:T(2,128)(2,1)}), bf16[8,2,192]{2,1,0:T(2,128)(2,1)S(1)}, u32[]{:S(2)}, u32[]{:S(2)}) async-start(bf16[8,2,192]{2,1,0:T(2,128)(2,1)} %reshape.130), calls=%async_computation.4 | async-start | bytes 16384 | tf_op jit(solution)/shard_map/all_to_all | solution.py:152
  109.8 2.1 %multiply_convert_fusion.1 = bf16[3,256,1024]{2,1,0:T(8,128)(2,1)S(1)} fusion(f32[3,256,1024]{2,1,0:T(8,128)S(1)} %get-tuple-element.37, bf16[256,3,128]{2,0,1:T(8,128)(2,1)} %copy.142, bf16[1024,3,128]{0,2,1:T(8,128)(2,1)} %bitcast.89, f32[3,256]{1,0:T(4,128)S(1)} %get-tuple-element.33, f32[3,256]{1,0:T(4,128)S(1)} %get-tuple-element.32), kind=kOutput, calls=%fused_computation.3 | convolution fusion | flops 204472320 | bytes 5707776 | tf_op jit(solution)/shard_map/qhd,khd->hqk/dot_general | solution.py:124
  114.7 2.0 %mul.66 = f32[32,8,384]{2,1,0:T(8,128)} reshape(f32[256,3,128]{2,1,0:T(4,128)} %copy.147) | data formatting | bytes 786432 | tf_op jit(solution)/shard_map/mul | solution.py:127
  116.7 1.8 %all-to-all-done.4 = bf16[8,2,192]{2,1,0:T(2,128)(2,1)S(1)} async-done(((bf16[8,2,192]{2,1,0:T(2,128)(2,1)}), bf16[8,2,192]{2,1,0:T(2,128)(2,1)S(1)}, u32[]{:S(2)}, u32[]{:S(2)}) %all-to-all-start.4) | async-done | bytes 6176 | tf_op jit(solution)/shard_map/all_to_all | solution.py:152
  118.5 5.1 %all-to-all-start.7 = ((f32[32,8,384]{2,1,0:T(8,128)}), f32[32,8,384]{2,1,0:T(8,128)S(1)}, u32[]{:S(2)}, u32[]{:S(2)}) async-start(f32[32,8,384]{2,1,0:T(8,128)} %mul.66), calls=%async_computation.7 | async-start | bytes 786432 | tf_op jit(solution)/shard_map/all_to_all | solution.py:25
  124.3 1.6 %fusion.4 = bf16[3,32,8,1024]{3,2,1,0:T(8,128)(2,1)} fusion(f32[3,256,1024]{2,1,0:T(8,128)S(1)} %get-tuple-element.37, f32[3,256]{1,0:T(4,128)S(1)} %get-tuple-element.32), kind=kLoop, calls=%fused_computation.10 | loop fusion | flops 1572864 | bytes 4721664 | tf_op jit(solution)/shard_map/reshape.10
  125.9 4.1 %fusion = bf16[3,1024,128]{2,1,0:T(8,128)(2,1)S(1)} fusion(bf16[3,32,8,1024]{3,2,1,0:T(8,128)(2,1)S(1)} %bitcast.90, bf16[32,8,3,128]{3,1,2,0:T(8,128)(2,1)S(1)} %bitcast.96), kind=kOutput, calls=%fused_computation.1 | convolution fusion | flops 210370560 | bytes 2555904 | tf_op jit(solution)/shard_map/hcbrk,cbrhd->bkhd/dot_general | solution.py:133
  130.0 7.7 %all-to-all-done.7 = f32[32,8,384]{2,1,0:T(8,128)S(1)} async-done(((f32[32,8,384]{2,1,0:T(8,128)}), f32[32,8,384]{2,1,0:T(8,128)S(1)}, u32[]{:S(2)}, u32[]{:S(2)}) %all-to-all-start.7) | async-done | bytes 393248 | tf_op jit(solution)/shard_map/all_to_all | solution.py:25
  139.0 6.3 %all-to-all-start.8 = ((bf16[8,2,192]{2,1,0:T(2,128)(2,1)}), bf16[8,2,192]{2,1,0:T(2,128)(2,1)S(1)}, u32[]{:S(2)}, u32[]{:S(2)}) async-start(bf16[8,2,192]{2,1,0:T(2,128)(2,1)} %reshape.132), calls=%async_computation.8 | async-start | bytes 16384 | tf_op jit(solution)/shard_map/all_to_all | solution.py:153
  145.3 4.0 %convert_reduce_fusion = bf16[3,1024,128]{2,1,0:T(8,128)(2,1)} fusion(bf16[3,32,8,1024]{3,2,1,0:T(8,128)(2,1)S(1)} %copy-done.4, bf16[32,8,3,128]{3,1,2,0:T(8,128)(2,1)S(1)} %bitcast.98), kind=kOutput, calls=%fused_computation.2 | convolution fusion | flops 207224832 | bytes 2555904 | tf_op jit(solution)/shard_map/hcbrk,cbrhd->bkhd/dot_general | solution.py:139
  152.3 2.0 %all-to-all-done.8 = bf16[8,2,192]{2,1,0:T(2,128)(2,1)S(1)} async-done(((bf16[8,2,192]{2,1,0:T(2,128)(2,1)}), bf16[8,2,192]{2,1,0:T(2,128)(2,1)S(1)}, u32[]{:S(2)}, u32[]{:S(2)}) %all-to-all-start.8) | async-done | bytes 6176 | tf_op jit(solution)/shard_map/all_to_all | solution.py:153
  (60 shorter events, 22.5 us)
Async XLA Ops:
  0.6 16.2 %copy-start = (f32[5,24]{1,0:T(8,128)S(1)}, f32[5,24]{1,0:T(8,128)}, u32[]{:S(2)}) copy-start(f32[5,24]{1,0:T(8,128)} %param.11) | copy-start | bytes 1444
  2.3 21.5 %all-to-all-start = ((bf16[32,8,384]{2,0,1:T(8,128)(2,1)}), bf16[32,8,384]{2,0,1:T(8,128)(2,1)S(1)}, u32[]{:S(2)}, u32[]{:S(2)}) async-start(bf16[32,8,384]{2,0,1:T(8,128)(2,1)} %bitcast.84), calls=%async_computation | async-start | bytes 393216 | tf_op jit(solution)/shard_map/all_to_all | solution.py:58
  23.8 0.7 copy-start.5
  27.1 17.8 %all-to-all-start.1 = ((f32[32,3,256]{2,1,0:T(4,128)}), f32[32,3,256]{2,1,0:T(4,128)S(1)}, u32[]{:S(2)}, u32[]{:S(2)}) async-start(f32[32,3,256]{2,1,0:T(4,128)} %broadcast_in_dim.16), calls=%async_computation.1 | async-start | bytes 262144 | tf_op jit(solution)/shard_map/all_to_all | solution.py:10
  44.9 13.4 %all-to-all-start.5 = ((bf16[32,8,384]{2,0,1:T(8,128)(2,1)}), bf16[32,8,384]{2,0,1:T(8,128)(2,1)S(1)}, u32[]{:S(2)}, u32[]{:S(2)}) async-start(bf16[32,8,384]{2,0,1:T(8,128)(2,1)} %bitcast.83), calls=%async_computation.5 | async-start | bytes 393216 | tf_op jit(solution)/shard_map/all_to_all | solution.py:59
  58.3 11.0 %copy-start.9 = (bf16[32,8,384]{2,0,1:T(8,128)(2,1)}, bf16[32,8,384]{2,0,1:T(8,128)(2,1)S(1)}, u32[]{:S(2)}) copy-start(bf16[32,8,384]{2,0,1:T(8,128)(2,1)S(1)} %all-to-all-done.5) | copy-start | bytes 589828
  58.3 13.9 %all-to-all-start.3 = ((f32[32,3,8]{2,1,0:T(4,128)}), f32[32,3,8]{2,1,0:T(4,128)S(1)}, u32[]{:S(2)}, u32[]{:S(2)}) async-start(f32[32,3,8]{2,1,0:T(4,128)} %copy.138), calls=%async_computation.3 | async-start | bytes 131072 | tf_op jit(solution)/shard_map/all_to_all | solution.py:25
  72.2 0.6 copy-start.10
  72.8 18.8 %all-to-all-start.2 = ((f32[32,8,384]{2,1,0:T(8,128)}), f32[32,8,384]{2,1,0:T(8,128)S(1)}, u32[]{:S(2)}, u32[]{:S(2)}) async-start(f32[32,8,384]{2,1,0:T(8,128)} %reshape_reshape.10), calls=%async_computation.2 | async-start | bytes 786432 | tf_op jit(solution)/shard_map/all_to_all | solution.py:25
  83.6 0.7 copy-start.11
  93.9 12.3 %all-to-all-start.6 = ((f32[32,8,6]{1,2,0:T(8,128)}), f32[32,8,6]{1,2,0:T(8,128)S(1)}, u32[]{:S(2)}, u32[]{:S(2)}) async-start(f32[32,8,6]{1,2,0:T(8,128)} %stack.2), calls=%async_computation.6 | async-start | bytes 262144 | tf_op jit(solution)/shard_map/all_to_all | solution.py:34
  106.3 12.2 %all-to-all-start.4 = ((bf16[8,2,192]{2,1,0:T(2,128)(2,1)}), bf16[8,2,192]{2,1,0:T(2,128)(2,1)S(1)}, u32[]{:S(2)}, u32[]{:S(2)}) async-start(bf16[8,2,192]{2,1,0:T(2,128)(2,1)} %reshape.130), calls=%async_computation.4 | async-start | bytes 16384 | tf_op jit(solution)/shard_map/all_to_all | solution.py:152
  109.7 3.3 %copy-start.3 = (bf16[1024,384]{0,1:T(8,128)(2,1)S(1)}, bf16[1024,384]{0,1:T(8,128)(2,1)}, u32[]{:S(2)}) copy-start(bf16[1024,384]{0,1:T(8,128)(2,1)} %copy.131) | copy-start | bytes 2359300
  111.9 1.2 copy-start.1
  118.5 19.2 %all-to-all-start.7 = ((f32[32,8,384]{2,1,0:T(8,128)}), f32[32,8,384]{2,1,0:T(8,128)S(1)}, u32[]{:S(2)}, u32[]{:S(2)}) async-start(f32[32,8,384]{2,1,0:T(8,128)} %mul.66), calls=%async_computation.7 | async-start | bytes 786432 | tf_op jit(solution)/shard_map/all_to_all | solution.py:25
  124.3 1.6 %copy-start.2 = (bf16[3,256,1024]{2,1,0:T(8,128)(2,1)S(1)}, bf16[3,256,1024]{2,1,0:T(8,128)(2,1)}, u32[]{:S(2)}) copy-start(bf16[3,256,1024]{2,1,0:T(8,128)(2,1)} %copy-done.1) | copy-start | bytes 4718596
  124.3 1.6 %copy-start.6 = (bf16[32,8,384]{2,1,0:T(8,128)(2,1)S(1)}, bf16[32,8,384]{2,1,0:T(8,128)(2,1)}, u32[]{:S(2)}) copy-start(bf16[32,8,384]{2,1,0:T(8,128)(2,1)} %copy-done.5) | copy-start | bytes 589828
  125.9 19.4 %copy-start.4 = (bf16[3,32,8,1024]{3,2,1,0:T(8,128)(2,1)S(1)}, bf16[3,32,8,1024]{3,2,1,0:T(8,128)(2,1)}, u32[]{:S(2)}) copy-start(bf16[3,32,8,1024]{3,2,1,0:T(8,128)(2,1)} %fusion.4) | copy-start | bytes 4718596
  125.9 19.4 %copy-start.7 = (bf16[32,8,384]{2,1,0:T(8,128)(2,1)S(1)}, bf16[32,8,384]{2,1,0:T(8,128)(2,1)}, u32[]{:S(2)}) copy-start(bf16[32,8,384]{2,1,0:T(8,128)(2,1)} %copy.184) | copy-start | bytes 589828
  139.0 15.3 %all-to-all-start.8 = ((bf16[8,2,192]{2,1,0:T(2,128)(2,1)}), bf16[8,2,192]{2,1,0:T(2,128)(2,1)S(1)}, u32[]{:S(2)}, u32[]{:S(2)}) async-start(bf16[8,2,192]{2,1,0:T(2,128)(2,1)} %reshape.132), calls=%async_computation.8 | async-start | bytes 16384 | tf_op jit(solution)/shard_map/all_to_all | solution.py:153
  149.4 1.5 copy-start.8
